TPU v7x, 128 devices: a whole 4x4x4 slice. The times are simulated.
128 devices in a mesh: group: 4 (over y), leaf: 32 (over x, z, core).
Axes of the slice: x: 4, y: 4, z: 4, core: 2. Of those that a mesh axis runs over, the one named last changes fastest.
Arguments:
- points: bfloat16 [262144, 64], P(('group', 'leaf')), may hold values from -1.1953125 to 1.1953125
- ordering: int32 [128, 2048], P(('group', 'leaf')), may hold values from 0 to 2047, each once within a row
- iterate: float32 [262144, 128], P(('group', 'leaf')), may hold values from -6 to 6
- target: float32 [262144, 128], P(('group', 'leaf')), may hold values from -18 to 18
- step_size: float32 [128], replicated, may hold values from 0.1 to 0.5
- leaf_basis: bfloat16 [262144, 256], P(('group', 'leaf')), may hold values from -0.125 to 0.125
- transfer: bfloat16 [128, 256, 256], P(('group', 'leaf')), may hold values from -0.375 to 0.375
- leaf_skeleton: bfloat16 [128, 256, 64], P(('group', 'leaf')), may hold values from -0.8984375 to 0.8984375
- cluster_skeleton: bfloat16 [4, 256, 64], P('group'), may hold values from -1.1953125 to 1.1953125
- near_table: int32 [128, 32], P(('group', 'leaf')), may hold values from 0 to 1, as said below
- far_table: int32 [128, 32], P(('group', 'leaf')), may hold values from 0 to 1, as said below
- cluster_far: int32 [4, 4], P('group'), may hold values from 0 to 1, as said below
Outputs:
- updated: float32 [262144, 128], P(('group', 'leaf'))
Inputs may be any that keep to these rules, and one draw needn't show every extreme that they name: `near_table`: entries 0 or 1; each leaf's own place is 1; a 1 stands only at places at most 3 away from the leaf's own place; each row has at most 7 ones, and some row exactly 7. `far_table`: entries 0 or 1, never 1 where near_table is 1. `cluster_far`: entries 0 or 1, zero on the diagonal. `ordering`: each row is a permutation.
All inputs are finite; a program needn't handle non-finite values.
Results may differ from a plain program's by a relative error of at most 0.0044.
Values may be sent and summed in bfloat16 or wider, within the bound.
A program may use at most 128 MiB of HBM per device.

v0:
```python
import jax
import jax.numpy as jnp
from jax import lax
from jax.experimental import pallas as pl
from jax.experimental.pallas import tpu as pltpu
from jax.sharding import PartitionSpec as P

LEAF, DIM, NRHS, RANK, CLUSTER, GROUPS = 2048, 64, 128, 256, 32, 4
HALF_LEAF = LEAF // 2
LANES = 128
CHUNKS = 4
QH = HALF_LEAF // CHUNKS
CHUNK_ROWS = 3 * QH
BLOCKS = QH // LANES
LOG2E = 1.4426950408889634
BIG = 1.0e4
POINT_SHIFT, LEAF_SHIFT, CLUSTER_SHIFT = 45.0, 25.0, 45.0
OWN, PARTNER, DOWN, UP, PARTNER_DOWN, PARTNER_UP, FAR_SIDE = range(7)
F32, BF16 = jnp.float32, jnp.bfloat16


def dot(a, b):
    return jnp.dot(a, b, preferred_element_type=F32)


def packed(rows):
    half = rows.shape[0] // 2
    return jnp.concatenate([rows[:half], rows[half:]], axis=1)


def stationary(pack_t, shift):
    doubled = pack_t + pack_t
    zeros = jnp.zeros_like(doubled[:DIM])
    low, high = doubled[:DIM], doubled[DIM:]
    both = jnp.concatenate([low, high], axis=1)
    empty = jnp.concatenate([zeros, zeros], axis=1)
    first = jnp.concatenate([both, empty], axis=0).astype(BF16)
    second = jnp.concatenate([empty, both], axis=0).astype(BF16)
    squares = pack_t * pack_t
    norm = jnp.concatenate(
        [jnp.sum(squares[:DIM], axis=0, keepdims=True), jnp.sum(squares[DIM:], axis=0, keepdims=True)],
        axis=1,
    )
    return first, second, (norm + shift) * LOG2E, jnp.exp2((shift - norm) * LOG2E)


def kernel(
    points, ordering, iterate, target, step, basis, transfer, leaf_skel, cluster_skel,
    near_table, far_table, cluster_far,
    out,
    nb, at, exponent, values, near, gathered, skel_at, skel_exp, far_acc,
    up_own, up_pair, up_z, up_x, yb, cluster_at, cluster_exp, low,
    near_send, near_recv, gat_send, gat_recv, up_send, up_recv, y_send, y_recv,
):
    g = lax.axis_index("group")
    l = lax.axis_index("leaf")
    x, z, k = l // 8, (l // 2) % 4, l % 2

    def at_leaf(xx, zz):
        return (xx % 4) * 8 + (zz % 4) * 2 + k

    partner = x * 8 + z * 2 + (1 - k)
    above, below = (l + 2) % CLUSTER, (l + CLUSTER - 2) % CLUSTER
    side = (l + CLUSTER + 2 * k - 1) % CLUSTER
    z_peers = [at_leaf(x, z + 1), at_leaf(x, z + 3), at_leaf(x, z + 2)]
    x_peers = [at_leaf(x + 1, z), at_leaf(x + 3, z), at_leaf(x + 2, z)]
    y_peers = [(g + 1) % GROUPS, (g + 3) % GROUPS, (g + 2) % GROUPS]

    barrier = pltpu.get_barrier_semaphore()
    for leaf in [partner, above, below, side] + z_peers + x_peers:
        pl.semaphore_signal(barrier, 1, device_id={"leaf": leaf}, device_id_type=pl.DeviceIdType.MESH)
    for group in y_peers:
        pl.semaphore_signal(barrier, 1, device_id={"group": group}, device_id_type=pl.DeviceIdType.MESH)

    def remote(src, dst, send, recv, leaf=None, group=None):
        return pltpu.make_async_remote_copy(
            src_ref=src, dst_ref=dst, send_sem=send, recv_sem=recv,
            device_id={"leaf": leaf} if group is None else {"group": group},
            device_id_type=pl.DeviceIdType.MESH,
        )

    for c in range(CHUNKS):
        rows = slice(c * QH, (c + 1) * QH)
        rows_high = slice(HALF_LEAF + c * QH, HALF_LEAF + (c + 1) * QH)
        nb[OWN, c, 0:QH, :] = jnp.concatenate([points[rows, :], points[rows_high, :]], axis=1)
    pack_t = jnp.concatenate(
        [nb[OWN, c, 0:QH, :].astype(F32).T for c in range(CHUNKS)], axis=1
    )
    first, second, exponent_row, scale = stationary(pack_t, POINT_SHIFT)
    at[0] = first
    at[1] = second
    exponent[...] = exponent_row
    for i in range(LEAF // LANES):
        block = iterate[i * LANES:(i + 1) * LANES, :].astype(BF16).astype(F32).T
        values[:, i * LANES:(i + 1) * LANES] = block.astype(BF16)
        high, j = divmod(i, HALF_LEAF // LANES)
        c, b = divmod(j, BLOCKS)
        start = QH + LANES * (high * BLOCKS + b)
        nb[OWN, c, start:start + LANES, :] = (
            block * scale[:, i * LANES:(i + 1) * LANES]
        ).astype(BF16)

    pl.semaphore_wait(barrier, 13)

    def near_copy(kind, c):
        src, dst, leaf = [
            (OWN, PARTNER, partner),
            (OWN, DOWN, above),
            (OWN, UP, below),
            (DOWN, PARTNER_DOWN, partner),
            (UP, PARTNER_UP, partner),
            (DOWN + 1 - k, FAR_SIDE, side),
        ][kind]
        return remote(nb.at[src, c], nb.at[dst, c], near_send.at[kind, c], near_recv.at[dst - 1, c], leaf)

    def send_near(kinds, c):
        for kind in kinds:
            near_copy(kind, c).start()

    def near_arrived(kinds, c):
        for kind in kinds:
            near_copy(kind, c).wait_recv()

    for c in range(CHUNKS):
        send_near([0], c)
    send_near([1, 2], 0)

    coef = dot(values[...], basis[...]).astype(BF16)
    skel_pack = packed(leaf_skel[0])
    first, second, exponent_row, scale = stationary(skel_pack.astype(F32).T, LEAF_SHIFT)
    skel_at[0] = first
    skel_at[1] = second
    skel_exp[...] = exponent_row
    scaled = (coef.astype(F32) * scale).astype(BF16)
    gathered[k, x, z, 0:LANES, :] = skel_pack
    gathered[k, x, z, LANES:2 * LANES, :] = scaled[:, :LANES]
    gathered[k, x, z, 2 * LANES:, :] = scaled[:, LANES:]
    z_from = [(z + 3) % 4, (z + 1) % 4, (z + 2) % 4]

    def gather_z(i):
        own = gathered.at[k, x, z]
        return remote(own, own, gat_send.at[i], gat_recv.at[i], z_peers[i])

    for i in range(3):
        gather_z(i).start()
    lifted = dot(coef, transfer[0])
    up_own[0] = lifted[:NRHS // 2]
    up_own[1] = lifted[NRHS // 2:]
    pair_copy = remote(up_own.at[1 - k], up_pair, up_send.at[0], up_recv.at[0], partner)
    pair_copy.start()
    send_near([1, 2], 1)

    near[...] = jnp.zeros_like(near)

    def near_chunk(slot, c, place):
        inside = (place >= 0) & (place < CLUSTER)
        listed = near_table[0, (place + CLUSTER) % CLUSTER] * inside.astype(jnp.int32)
        row = exponent[...] + (1.0 - listed.astype(F32)) * BIG
        points_c = nb[slot, c, 0:QH, :]

        def weights(h):
            s = dot(points_c, at[h])
            return jnp.exp2(s * LOG2E - row).astype(BF16)

        def value(h):
            start = QH + h * BLOCKS * LANES
            return jnp.concatenate(
                [nb[slot, c, start + b * LANES:start + (b + 1) * LANES, :] for b in range(BLOCKS)], axis=1
            )

        low_w = weights(0)
        high_w = weights(1)
        near[...] += dot(value(0), low_w)
        near[...] += dot(value(1), high_w)

    def whole(slot, place):
        def visit(c, carry):
            near_chunk(slot, c, place)
            return carry

        lax.fori_loop(0, CHUNKS, visit, 0)

    def stage(c):
        near_arrived([3, 4], c)

        def visit(slot, carry):
            other = jnp.where(slot >= PARTNER_DOWN, l + 1 - 2 * k, l)
            place = other + 4 * (slot % 2) - 2
            near_chunk(slot, c, place)
            return carry

        lax.fori_loop(DOWN, PARTNER_UP + 1, visit, 0)

    def forward(c):
        near_arrived([1, 2], c)
        send_near([3, 4, 5], c)

    whole(OWN, l)

    pair_copy.wait_recv()
    up_z[0] = up_own[k] + up_pair[...]

    def up_copy_z(i):
        return remote(up_z.at[0], up_z.at[i + 1], up_send.at[1 + i], up_recv.at[1 + i], z_peers[i])

    def up_copy_x(i):
        return remote(up_x.at[0], up_x.at[i + 1], up_send.at[4 + i], up_recv.at[4 + i], x_peers[i])

    for i in range(3):
        up_copy_z(i).start()

    def gather_x(i):
        own = gathered.at[k, x]
        return remote(own, own, gat_send.at[3 + i], gat_recv.at[3 + i], x_peers[i])

    def gather_relay(i):
        column = (x + 3) % 4 if i == 0 else (x + 1) % 4
        part = gathered.at[k, column, pl.ds(2 * i, 2)]
        return remote(part, part, gat_send.at[5 + i], gat_recv.at[5 + i], x_peers[i])

    def gather_pair(i):
        column = (x + i) % 4
        part = gathered.at[k, column]
        return remote(part, part, gat_send.at[7 + i], gat_recv.at[7 + i], partner)

    for i in range(3):
        gather_z(i).wait_recv()
    for i in range(2):
        gather_x(i).start()
    gather_pair(0).start()
    send_near([1, 2], 2)
    forward(0)
    near_arrived([0], 0)
    near_arrived([0], 1)
    near_arrived([0], 2)
    near_arrived([0], 3)
    whole(PARTNER, l + 1 - 2 * k)

    send_near([1, 2], 3)
    forward(1)
    for i in range(3):
        up_copy_z(i).wait_recv()
    up_x[0] = (up_z[0] + up_z[1]) + (up_z[2] + up_z[3])
    for i in range(3):
        up_copy_x(i).start()
    stage(0)

    forward(2)
    for i in range(2):
        gather_x(i).wait_recv()
    for i in range(2):
        gather_relay(i).start()
    gather_pair(1).start()
    gather_pair(3).start()
    for i in range(3):
        up_copy_x(i).wait_recv()
    upper = ((up_x[0] + up_x[1]) + (up_x[2] + up_x[3])).astype(BF16)
    cluster_pack = packed(cluster_skel[0])
    first, second, exponent_row, scale = stationary(cluster_pack.astype(F32).T, CLUSTER_SHIFT)
    cluster_at[0] = first
    cluster_at[1] = second
    cluster_exp[...] = exponent_row
    scaled = (upper.astype(F32) * scale).astype(BF16)
    yb[g, 0:LANES, :] = cluster_pack
    yb[g, LANES:LANES + NRHS // 2, :] = scaled[:, :LANES]
    yb[g, LANES + NRHS // 2:, :] = scaled[:, LANES:]

    def y_copy(i):
        return remote(yb.at[g], yb.at[g], y_send.at[i], y_recv.at[i], group=y_peers[i])

    for i in range(3):
        y_copy(i).start()
    stage(1)

    forward(3)
    for i in range(3):
        y_copy(i).wait_recv()

    def block_weights(pack, stationary_ref, row):
        return jnp.concatenate(
            [jnp.exp2(dot(pack, stationary_ref[h]) * LOG2E - row).astype(BF16) for h in range(2)], axis=0
        )

    lower = jnp.zeros((NRHS // 2, RANK), F32)
    for h in range(GROUPS):
        row = cluster_exp[...] + (1.0 - cluster_far[0, h].astype(F32)) * BIG
        weights = block_weights(yb[h, 0:LANES, :], cluster_at, row)
        value = jnp.concatenate(
            [yb[h, LANES:LANES + NRHS // 2, :], yb[h, LANES + NRHS // 2:, :]], axis=1
        )
        lower = lower + dot(value, weights)
    low[k] = lower.astype(BF16)
    low_copy = remote(low.at[k], low.at[k], y_send.at[3], y_recv.at[3], partner)
    low_copy.start()
    stage(2)

    for i in range(2):
        gather_relay(i).wait_recv()
    gather_pair(2).start()
    stage(3)

    for i in range(4):
        gather_pair(i).wait_recv()
    far_acc[...] = jnp.zeros_like(far_acc)

    def far_visit(n, carry):
        kk, xx = n // 4, n % 4
        total = jnp.zeros((NRHS, RANK), F32)
        for zz in range(4):
            row = skel_exp[...] + (1.0 - far_table[0, xx * 8 + zz * 2 + kk].astype(F32)) * BIG
            weights = block_weights(gathered[kk, xx, zz, 0:LANES, :], skel_at, row)
            value = jnp.concatenate(
                [gathered[kk, xx, zz, LANES:2 * LANES, :], gathered[kk, xx, zz, 2 * LANES:, :]], axis=1
            )
            total = total + dot(value, weights)
        far_acc[...] += total
        return carry

    lax.fori_loop(0, 8, far_visit, 0)
    low_copy.wait_recv()
    lower_all = jnp.concatenate([low[0], low[1]], axis=0)
    local_t = far_acc[...] + lax.dot_general(
        lower_all, transfer[0], (((1,), (1,)), ((), ())), preferred_element_type=F32
    )
    local = local_t.astype(BF16).astype(F32).T.astype(BF16)

    def pick(i, carry):
        for j in range(8):
            out[pl.ds(i * 8 + j, 1), :] = target[pl.ds(ordering[0, i * 8 + j], 1), :]
        return carry

    lax.fori_loop(0, LEAF // 8, pick, 0)

    def last(c, carry):
        near_copy(5, c).wait_recv()
        near_chunk(FAR_SIDE, c, l + 6 * k - 3)
        return carry

    lax.fori_loop(0, CHUNKS, last, 0)
    for i in range(LEAF // LANES):
        rows = slice(i * LANES, (i + 1) * LANES)
        image = dot(basis[rows, :], local) + near[:, rows].T
        out[rows, :] = iterate[rows, :] + step[...] * (out[rows, :] - image)

    for kind in range(6):
        for c in range(CHUNKS):
            near_copy(kind, c).wait_send()
    for i in range(3):
        gather_z(i).wait_send()
        up_copy_z(i).wait_send()
        up_copy_x(i).wait_send()
        y_copy(i).wait_send()
    for i in range(2):
        gather_x(i).wait_send()
        gather_relay(i).wait_send()
    for i in range(4):
        gather_pair(i).wait_send()
    pair_copy.wait_send()
    low_copy.wait_send()


def body(
    points, ordering, iterate, target, step_size, leaf_basis, transfer, leaf_skeleton,
    cluster_skeleton, near_table, far_table, cluster_far,
):
    vmem = pl.BlockSpec(memory_space=pltpu.VMEM)
    smem = pl.BlockSpec(memory_space=pltpu.SMEM)
    dma = pltpu.SemaphoreType.DMA
    return pl.pallas_call(
        kernel,
        out_shape=jax.ShapeDtypeStruct((LEAF, NRHS), F32),
        in_specs=[vmem, smem, vmem, vmem, vmem, vmem, vmem, vmem, vmem, smem, smem, smem],
        out_specs=vmem,
        scratch_shapes=[
            pltpu.VMEM((7, CHUNKS, CHUNK_ROWS, LANES), BF16),
            pltpu.VMEM((2, LANES, LEAF), BF16),
            pltpu.VMEM((1, LEAF), F32),
            pltpu.VMEM((NRHS, LEAF), BF16),
            pltpu.VMEM((NRHS, LEAF), F32),
            pltpu.VMEM((2, 4, 4, 3 * LANES, LANES), BF16),
            pltpu.VMEM((2, LANES, RANK), BF16),
            pltpu.VMEM((1, RANK), F32),
            pltpu.VMEM((NRHS, RANK), F32),
            pltpu.VMEM((2, NRHS // 2, RANK), F32),
            pltpu.VMEM((NRHS // 2, RANK), F32),
            pltpu.VMEM((4, NRHS // 2, RANK), F32),
            pltpu.VMEM((4, NRHS // 2, RANK), F32),
            pltpu.VMEM((GROUPS, LANES + NRHS, LANES), BF16),
            pltpu.VMEM((2, LANES, RANK), BF16),
            pltpu.VMEM((1, RANK), F32),
            pltpu.VMEM((2, NRHS // 2, RANK), BF16),
            dma((6, CHUNKS)), dma((6, CHUNKS)),
            dma((11,)), dma((11,)),
            dma((7,)), dma((7,)),
            dma((4,)), dma((4,)),
        ],
        compiler_params=pltpu.CompilerParams(
            collective_id=0, has_side_effects=True, vmem_limit_bytes=56 * 2**20
        ),
    )(
        points, ordering, iterate, target, step_size[None, :], leaf_basis, transfer,
        leaf_skeleton, cluster_skeleton, near_table, far_table, cluster_far,
    )


def solution(mesh):
    both = ("group", "leaf")
    return jax.shard_map(
        body,
        mesh=mesh,
        in_specs=(
            P(both, None), P(both, None), P(both, None), P(both, None), P(), P(both, None),
            P(both, None, None), P(both, None, None), P("group", None, None),
            P(both, None), P(both, None), P("group", None),
        ),
        out_specs=P(both, None),
        check_vma=False,
    )
```

profile of v0, /device:TPU:2, one launch (start us, length us, event | category | flops | bytes accessed | tf_op | source)
XLA Modules:
  0.0 86.0 jit_solution(15965611074161487756)
XLA Ops:
  0.0 0.0 copy-start
  0.0 1.5 %copy.14.leaf_skel = bf16[1,256,64]{2,1,0:T(8,128)(2,1)} copy(bf16[1,256,64]{1,2,0:T(8,128)(2,1)} %param.19) | data formatting | bytes 65536 | tf_op args[7]
  1.5 0.0 copy-done
  1.5 0.7 copy.15.cluster_skel
  2.2 2.0 %copy.13.points = bf16[2048,64]{1,0:T(8,128)(2,1)} copy(bf16[2048,64]{0,1:T(8,128)(2,1)} %param.12) | data formatting | bytes 524288 | tf_op args[0]
  4.2 79.6 %shard_map.118 = f32[2048,128]{1,0:T(8,128)} custom-call(bf16[2048,64]{1,0:T(8,128)(2,1)} %copy.13.points, s32[1,2048]{1,0:T(1,128)} %ordering.1, f32[2048,128]{1,0:T(8,128)} %iterate.1, f32[2048,128]{1,0:T(8,128)} %target.1, f32[1,128]{1,0:T(1,128)} %bitcast.1, bf16[2048,256]{1,0:T(8,128)(2,1)} %basis.1, bf16[1,256,256]{2,1,0:T(8,128)(2,1)} %transfer.1, ...), custom_call_target="tpu_custom_call" | custom-call | tf_op jit(solution)/shard_map/pallas_call | solution.py:369
  83.8 2.3 %copy.17 = f32[2048,128]{1,0:T(8,128)} copy(f32[2048,128]{1,0:T(8,128)} %shard_map.118) | data formatting | bytes 2097152
Async XLA Ops:
  0.0 1.5 %copy-start = (bf16[1,256,64]{1,2,0:T(8,128)(2,1)S(1)}, bf16[1,256,64]{1,2,0:T(8,128)(2,1)}, u32[]{:S(2)}) copy-start(bf16[1,256,64]{1,2,0:T(8,128)(2,1)} %param.20) | copy-start | bytes 98308
where the time goes:
time: 86.3 us; the launch traced here: 86 us
  Pallas kernels  79.6 us (92%)
  local copies, waits for them, and re-layouts  6.44 us (7%)
    pallas_call x1, Pallas kernels, body(): pl.pallas_call(kernel, out_shape=jax.ShapeDtypeStruct((LEAF, NRHS), F32),...  79.6 us
    unnamed x6, local copies, waits for them, and re-layouts  6.44 us

commit v1 on v0

v1 whole, which is shorter than its diff:
```python
import jax
import jax.numpy as jnp
from jax import lax
from jax.experimental import pallas as pl
from jax.experimental.pallas import tpu as pltpu
from jax.sharding import PartitionSpec as P

LEAF, DIM, NRHS, RANK, CLUSTER, GROUPS = 2048, 64, 128, 256, 32, 4
HALF_LEAF = LEAF // 2
LANES = 128
CHUNKS = 4
QH = HALF_LEAF // CHUNKS
CHUNK_ROWS = 3 * QH
BLOCKS = QH // LANES
LOG2E = 1.4426950408889634
BIG = 1.0e4
POINT_SHIFT, LEAF_SHIFT, CLUSTER_SHIFT = 45.0, 25.0, 45.0
OWN, PARTNER, DOWN, UP, PARTNER_DOWN, PARTNER_UP, FAR_SIDE = range(7)
F32, BF16 = jnp.float32, jnp.bfloat16


def dot(a, b):
    return jnp.dot(a, b, preferred_element_type=F32)


def stacked(cols):
    half = cols.shape[1] // 2
    return jnp.concatenate([cols[:, :half], cols[:, half:]], axis=0)


def exponent_and_scale(cols, shift):
    norm = jnp.sum(cols * cols, axis=0, keepdims=True)
    return (norm + shift) * LOG2E, jnp.exp2((shift - norm) * LOG2E)


def fill_stationary(ref, doubled):
    zeros = jnp.zeros_like(doubled)
    ref[0, 0:DIM, :] = doubled
    ref[0, DIM:, :] = zeros
    ref[1, 0:DIM, :] = zeros
    ref[1, DIM:, :] = doubled


def kernel(
    points, ordering, iterate, target, step, basis, transfer, leaf_skel, cluster_skel,
    near_table, far_table, cluster_far,
    out,
    nb, at, exponent, values, near, gathered, row_skel, row_exp, own_exp, row_at, far_total, far_out, far_in,
    up_total, up_out, up_in, yb, cluster_at, cluster_exp, low,
    near_send, near_recv, gat_send, gat_recv, row_send, row_recv, up_send, up_recv, y_send, y_recv,
):
    g = lax.axis_index("group")
    l = lax.axis_index("leaf")
    x, z, k = l // 8, (l // 2) % 4, l % 2
    half = NRHS // 2

    def at_leaf(xx, zz):
        return (xx % 4) * 8 + (zz % 4) * 2 + k

    partner = x * 8 + z * 2 + (1 - k)
    above, below = (l + 2) % CLUSTER, (l + CLUSTER - 2) % CLUSTER
    side = (l + CLUSTER + 2 * k - 1) % CLUSTER
    z_even, x_even = z % 2, x % 2
    z_first, z_second = at_leaf(x, z + 1 - 2 * z_even), at_leaf(x, z + 3 + 2 * z_even)
    x_first, x_second = at_leaf(x + 1 - 2 * x_even, z), at_leaf(x + 3 + 2 * x_even, z)
    x_peers = [at_leaf(x + i, z) for i in range(1, 4)]
    y_peers = [(g + i) % GROUPS for i in range(1, 4)]

    barrier = pltpu.get_barrier_semaphore()
    for leaf in [partner, above, below, side, z_first, z_second] + x_peers:
        pl.semaphore_signal(barrier, 1, device_id={"leaf": leaf}, device_id_type=pl.DeviceIdType.MESH)
    for group in y_peers:
        pl.semaphore_signal(barrier, 1, device_id={"group": group}, device_id_type=pl.DeviceIdType.MESH)

    def remote(src, dst, send, recv, leaf=None, group=None):
        return pltpu.make_async_remote_copy(
            src_ref=src, dst_ref=dst, send_sem=send, recv_sem=recv,
            device_id={"leaf": leaf} if group is None else {"group": group},
            device_id_type=pl.DeviceIdType.MESH,
        )

    cols = points[...].astype(F32)
    stack = stacked(cols)
    for c in range(CHUNKS):
        nb[OWN, c, 0:QH, :] = stack[:, c * QH:(c + 1) * QH].T.astype(BF16)
    fill_stationary(at, (cols + cols).astype(BF16))
    exponent_row, scale = exponent_and_scale(cols, POINT_SHIFT)
    exponent[...] = exponent_row
    for i in range(LEAF // LANES):
        block = iterate[i * LANES:(i + 1) * LANES, :].astype(BF16).astype(F32).T
        values[:, i * LANES:(i + 1) * LANES] = block.astype(BF16)
        high, j = divmod(i, HALF_LEAF // LANES)
        c, b = divmod(j, BLOCKS)
        start = QH + LANES * (high * BLOCKS + b)
        nb[OWN, c, start:start + LANES, :] = (
            block * scale[:, i * LANES:(i + 1) * LANES]
        ).astype(BF16)

    pl.semaphore_wait(barrier, 12)

    def near_copy(kind, c):
        src, dst, leaf = [
            (OWN, PARTNER, partner),
            (OWN, DOWN, above),
            (OWN, UP, below),
            (DOWN, PARTNER_DOWN, partner),
            (UP, PARTNER_UP, partner),
            (DOWN + 1 - k, FAR_SIDE, side),
        ][kind]
        return remote(nb.at[src, c], nb.at[dst, c], near_send.at[kind, c], near_recv.at[dst - 1, c], leaf)

    def send_near(kinds, c):
        for kind in kinds:
            near_copy(kind, c).start()

    def near_arrived(kinds, c):
        for kind in kinds:
            near_copy(kind, c).wait_recv()

    send_near([1, 2], 0)
    for c in range(CHUNKS):
        send_near([0], c)

    coef = dot(values[...], basis[...]).astype(BF16)
    skel = leaf_skel[0].astype(F32)
    skel_row, scale = exponent_and_scale(skel, LEAF_SHIFT)
    scaled = (coef.astype(F32) * scale).astype(BF16)
    gathered[k, z, 0:LANES, :] = stacked(skel).T.astype(BF16)
    gathered[k, z, LANES:2 * LANES, :] = scaled[:, :LANES]
    gathered[k, z, 2 * LANES:, :] = scaled[:, LANES:]

    def gather_copy(i):
        part = [gathered.at[k, z], gathered.at[k, pl.ds(2 * (z // 2), 2)], gathered.at[k]][i]
        return remote(part, part, gat_send.at[i], gat_recv.at[i], [z_first, z_second, partner][i])

    gather_copy(0).start()
    lifted = dot(coef, transfer[0])
    for i in range(2):
        up_total[i] = lifted[i * half:(i + 1) * half]
        up_out[i] = lifted[i * half:(i + 1) * half].astype(BF16)

    def up_copy(i):
        src = up_out.at[1 - k] if i == 0 else up_out.at[i + 1]
        leaf = [partner, z_first, z_second, x_first, x_second][i]
        return remote(src, up_in.at[i], up_send.at[i], up_recv.at[i], leaf)

    up_copy(0).start()

    row_skel[x] = (skel + skel).astype(BF16)
    for xx in range(4):
        for j in range(8):
            own_exp[xx, j:j + 1, :] = skel_row + (1.0 - far_table[0, xx * 8 + j].astype(F32)) * BIG
    row_exp[x] = own_exp[x]

    def row_copies(i):
        leaf, there = x_peers[i - 1], (x + i) % 4
        return [
            remote(row_skel.at[x], row_skel.at[x], row_send.at[0, i - 1], row_recv.at[0, i - 1], leaf),
            remote(own_exp.at[there], row_exp.at[x], row_send.at[1, i - 1], row_recv.at[1, i - 1], leaf),
        ]

    def far_copy(i):
        return remote(
            far_out.at[i - 1], far_in.at[i - 1], row_send.at[2, i - 1], row_recv.at[2, i - 1], x_peers[i - 1]
        )

    for i in range(1, 4):
        for copy in row_copies(i):
            copy.start()
    send_near([1, 2], 1)

    near[...] = jnp.zeros_like(near)

    def near_chunk(slot, c, place):
        inside = (place >= 0) & (place < CLUSTER)
        listed = near_table[0, (place + CLUSTER) % CLUSTER] * inside.astype(jnp.int32)
        row = exponent[...] + (1.0 - listed.astype(F32)) * BIG
        points_c = nb[slot, c, 0:QH, :]

        def weights(h):
            s = dot(points_c, at[h])
            return jnp.exp2(s * LOG2E - row).astype(BF16)

        def value(h):
            start = QH + h * BLOCKS * LANES
            return jnp.concatenate(
                [nb[slot, c, start + b * LANES:start + (b + 1) * LANES, :] for b in range(BLOCKS)], axis=1
            )

        low_w = weights(0)
        high_w = weights(1)
        near[...] += dot(value(0), low_w)
        near[...] += dot(value(1), high_w)

    def some(slot, place, start, stop):
        def visit(c, carry):
            near_chunk(slot, c, place)
            return carry

        lax.fori_loop(start, stop, visit, 0)

    def stage(c):
        near_arrived([3, 4], c)

        def visit(slot, carry):
            other = jnp.where(slot >= PARTNER_DOWN, l + 1 - 2 * k, l)
            place = other + 4 * (slot % 2) - 2
            near_chunk(slot, c, place)
            return carry

        lax.fori_loop(DOWN, PARTNER_UP + 1, visit, 0)

    def forward(c):
        near_arrived([1, 2], c)
        send_near([3, 4, 5], c)

    def add_up(i):
        up_copy(i).wait_recv()
        total = (up_total[k] if i == 0 else up_total[0]) + up_in[i].astype(F32)
        up_total[0] = total
        if i < 4:
            up_out[i + 2] = total.astype(BF16)
            up_copy(i + 1).start()
        return total

    some(OWN, l, 0, 2)
    add_up(0)
    some(OWN, l, 2, 4)
    gather_copy(0).wait_recv()
    gather_copy(1).start()
    near_arrived([0], 0)
    near_arrived([0], 1)
    some(PARTNER, l + 1 - 2 * k, 0, 2)
    add_up(1)
    send_near([1, 2], 2)
    forward(0)
    near_arrived([0], 2)
    near_arrived([0], 3)
    some(PARTNER, l + 1 - 2 * k, 2, 3)
    stage(0)

    add_up(2)
    gather_copy(1).wait_recv()
    gather_copy(2).start()
    send_near([1, 2], 3)
    forward(1)
    some(PARTNER, l + 1 - 2 * k, 3, 4)
    stage(1)

    add_up(3)
    forward(2)
    gather_copy(2).wait_recv()
    for i in range(1, 4):
        for copy in row_copies(i):
            copy.wait_recv()

    def far_visit(i, carry):
        there = (x + i) % 4
        fill_stationary(row_at, row_skel[there])
        rows = row_exp[there]
        items = [(zz, kk) for zz in range(4) for kk in range(2)]
        packs = jnp.concatenate([gathered[kk, zz, 0:LANES, :] for zz, kk in items], axis=0)
        total = jnp.zeros((NRHS, RANK), F32)
        for h in range(2):
            s = dot(packs, row_at[h]) * LOG2E
            weights = jnp.concatenate(
                [jnp.exp2(s[j * LANES:(j + 1) * LANES] - rows[j:j + 1]).astype(BF16) for j in range(8)], axis=0
            )
            value = jnp.concatenate(
                [gathered[kk, zz, (1 + h) * LANES:(2 + h) * LANES, :] for zz, kk in items], axis=1
            )
            total = total + dot(value, weights)
        far_total[i] = total
        return carry

    lax.fori_loop(0, 4, far_visit, 0)
    for i in range(1, 4):
        far_out[i - 1] = far_total[i].astype(BF16)
        far_copy(i).start()
    stage(2)

    upper = add_up(4).astype(BF16)
    cluster_cols = cluster_skel[0].astype(F32)
    fill_stationary(cluster_at, (cluster_cols + cluster_cols).astype(BF16))
    cluster_row, scale = exponent_and_scale(cluster_cols, CLUSTER_SHIFT)
    cluster_exp[...] = cluster_row
    scaled = (upper.astype(F32) * scale).astype(BF16)
    yb[g, 0:LANES, :] = stacked(cluster_cols).T.astype(BF16)
    yb[g, LANES:LANES + half, :] = scaled[:, :LANES]
    yb[g, LANES + half:, :] = scaled[:, LANES:]

    def y_copy(i):
        return remote(yb.at[g], yb.at[g], y_send.at[i], y_recv.at[i], group=y_peers[i])

    for i in range(3):
        y_copy(i).start()
    forward(3)

    def pick(i, carry):
        for j in range(8):
            out[pl.ds(i * 8 + j, 1), :] = target[pl.ds(ordering[0, i * 8 + j], 1), :]
        return carry

    lax.fori_loop(0, LEAF // 8, pick, 0)
    for i in range(3):
        y_copy(i).wait_recv()
    lower = jnp.zeros((half, RANK), F32)
    for h in range(GROUPS):
        row = cluster_exp[...] + (1.0 - cluster_far[0, h].astype(F32)) * BIG
        weights = jnp.concatenate(
            [jnp.exp2(dot(yb[h, 0:LANES, :], cluster_at[i]) * LOG2E - row).astype(BF16) for i in range(2)], axis=0
        )
        value = jnp.concatenate([yb[h, LANES:LANES + half, :], yb[h, LANES + half:, :]], axis=1)
        lower = lower + dot(value, weights)
    low[k] = lower.astype(BF16)
    low_copy = remote(low.at[k], low.at[k], y_send.at[3], y_recv.at[3], partner)
    low_copy.start()
    stage(3)

    for i in range(1, 4):
        far_copy(i).wait_recv()
    low_copy.wait_recv()
    lower_all = jnp.concatenate([low[0], low[1]], axis=0)
    far_sum = (far_total[0] + far_in[0].astype(F32)) + (far_in[1].astype(F32) + far_in[2].astype(F32))
    local_t = far_sum + lax.dot_general(
        lower_all, transfer[0], (((1,), (1,)), ((), ())), preferred_element_type=F32
    )
    local = local_t.astype(BF16).astype(F32).T.astype(BF16)

    def last(c, carry):
        near_copy(5, c).wait_recv()
        near_chunk(FAR_SIDE, c, l + 6 * k - 3)
        return carry

    lax.fori_loop(0, CHUNKS, last, 0)
    for i in range(LEAF // LANES):
        rows = slice(i * LANES, (i + 1) * LANES)
        image = dot(basis[rows, :], local) + near[:, rows].T
        out[rows, :] = iterate[rows, :] + step[...] * (out[rows, :] - image)

    for kind in range(6):
        for c in range(CHUNKS):
            near_copy(kind, c).wait_send()
    for i in range(3):
        gather_copy(i).wait_send()
        y_copy(i).wait_send()
        far_copy(i + 1).wait_send()
        for copy in row_copies(i + 1):
            copy.wait_send()
    for i in range(5):
        up_copy(i).wait_send()
    low_copy.wait_send()


def body(
    points, ordering, iterate, target, step_size, leaf_basis, transfer, leaf_skeleton,
    cluster_skeleton, near_table, far_table, cluster_far,
):
    vmem = pl.BlockSpec(memory_space=pltpu.VMEM)
    smem = pl.BlockSpec(memory_space=pltpu.SMEM)
    dma = pltpu.SemaphoreType.DMA
    return pl.pallas_call(
        kernel,
        out_shape=jax.ShapeDtypeStruct((LEAF, NRHS), F32),
        in_specs=[vmem, smem, vmem, vmem, vmem, vmem, vmem, vmem, vmem, smem, smem, smem],
        out_specs=vmem,
        scratch_shapes=[
            pltpu.VMEM((7, CHUNKS, CHUNK_ROWS, LANES), BF16),
            pltpu.VMEM((2, LANES, LEAF), BF16),
            pltpu.VMEM((1, LEAF), F32),
            pltpu.VMEM((NRHS, LEAF), BF16),
            pltpu.VMEM((NRHS, LEAF), F32),
            pltpu.VMEM((2, 4, 3 * LANES, LANES), BF16),
            pltpu.VMEM((4, DIM, RANK), BF16),
            pltpu.VMEM((4, 8, RANK), F32),
            pltpu.VMEM((4, 8, RANK), F32),
            pltpu.VMEM((2, LANES, RANK), BF16),
            pltpu.VMEM((4, NRHS, RANK), F32),
            pltpu.VMEM((3, NRHS, RANK), BF16),
            pltpu.VMEM((3, NRHS, RANK), BF16),
            pltpu.VMEM((2, NRHS // 2, RANK), F32),
            pltpu.VMEM((6, NRHS // 2, RANK), BF16),
            pltpu.VMEM((5, NRHS // 2, RANK), BF16),
            pltpu.VMEM((GROUPS, LANES + NRHS, LANES), BF16),
            pltpu.VMEM((2, LANES, RANK), BF16),
            pltpu.VMEM((1, RANK), F32),
            pltpu.VMEM((2, NRHS // 2, RANK), BF16),
            dma((6, CHUNKS)), dma((6, CHUNKS)),
            dma((3,)), dma((3,)),
            dma((3, 3)), dma((3, 3)),
            dma((5,)), dma((5,)),
            dma((4,)), dma((4,)),
        ],
        compiler_params=pltpu.CompilerParams(
            collective_id=0, has_side_effects=True, vmem_limit_bytes=56 * 2**20
        ),
    )(
        points.T, ordering, iterate, target, step_size[None, :], leaf_basis, transfer,
        leaf_skeleton.swapaxes(1, 2), cluster_skeleton.swapaxes(1, 2), near_table, far_table, cluster_far,
    )


def solution(mesh):
    both = ("group", "leaf")
    return jax.shard_map(
        body,
        mesh=mesh,
        in_specs=(
            P(both, None), P(both, None), P(both, None), P(both, None), P(), P(both, None),
            P(both, None, None), P(both, None, None), P("group", None, None),
            P(both, None), P(both, None), P("group", None),
        ),
        out_specs=P(both, None),
        check_vma=False,
    )
```

time: 86.3 us -> 65.5 us (0.76)
  the two profiles are of different devices: /device:TPU:2 before, /device:TPU:1 now
where the time goes in v1:
time: 65.5 us; the launch traced here: 65.3 us
  Pallas kernels  63.1 us (96%)
  local copies, waits for them, and re-layouts  2.26 us (3%)
    pallas_call x1, Pallas kernels, body(): pl.pallas_call(kernel, out_shape=jax.ShapeDtypeStruct((LEAF, NRHS), F32),...  63.1 us
    unnamed x1, local copies, waits for them, and re-layouts  2.26 us

profile of v1, /device:TPU:1, one launch (start us, length us, event | category | flops | bytes accessed | tf_op | source)
XLA Modules:
  0.0 65.3 jit_solution(3881077068092536562)
XLA Ops:
  0.0 63.1 %shard_map.118 = f32[2048,128]{1,0:T(8,128)} custom-call(bf16[64,2048]{1,0:T(8,128)(2,1)} %bitcast.4, s32[1,2048]{1,0:T(1,128)} %ordering.1, f32[2048,128]{1,0:T(8,128)} %iterate.1, f32[2048,128]{1,0:T(8,128)} %target.1, f32[1,128]{1,0:T(1,128)} %bitcast.7, bf16[2048,256]{1,0:T(8,128)(2,1)} %basis.1, bf16[1,256,256]{2,1,0:T(8,128)(2,1)} %transfer.1, ...), custom_call_target="tpu_custom_call" | custom-call | tf_op jit(solution)/shard_map/pallas_call | solution.py:362
  63.1 2.3 %copy.14 = f32[2048,128]{1,0:T(8,128)} copy(f32[2048,128]{1,0:T(8,128)} %shard_map.118) | data formatting | bytes 2097152

commit v2 on v1

--- a/solution.py
+++ b/solution.py
@@ -167,7 +167,6 @@
     for i in range(1, 4):
         for copy in row_copies(i):
             copy.start()
-    send_near([1, 2], 1)
 
     near[...] = jnp.zeros_like(near)
 
@@ -200,19 +199,16 @@
         lax.fori_loop(start, stop, visit, 0)
 
     def stage(c):
-        near_arrived([3, 4], c)
-
         def visit(slot, carry):
-            other = jnp.where(slot >= PARTNER_DOWN, l + 1 - 2 * k, l)
-            place = other + 4 * (slot % 2) - 2
-            near_chunk(slot, c, place)
+            center = jnp.where(slot >= PARTNER_DOWN, l + 1 - 2 * k, l)
+            near_chunk(slot, c, center + 4 * (slot % 2) - 2)
             return carry
 
-        lax.fori_loop(DOWN, PARTNER_UP + 1, visit, 0)
-
-    def forward(c):
         near_arrived([1, 2], c)
         send_near([3, 4, 5], c)
+        lax.fori_loop(DOWN, PARTNER_DOWN, visit, 0)
+        near_arrived([3, 4], c)
+        lax.fori_loop(PARTNER_DOWN, FAR_SIDE, visit, 0)
 
     def add_up(i):
         up_copy(i).wait_recv()
@@ -223,32 +219,33 @@
             up_copy(i + 1).start()
         return total
 
-    some(OWN, l, 0, 2)
+    other = l + 1 - 2 * k
+    some(OWN, l, 0, 4)
     add_up(0)
-    some(OWN, l, 2, 4)
+    send_near([1, 2], 1)
+    near_arrived([0], 0)
+    near_arrived([0], 1)
+    some(PARTNER, other, 0, 2)
     gather_copy(0).wait_recv()
     gather_copy(1).start()
-    near_arrived([0], 0)
-    near_arrived([0], 1)
-    some(PARTNER, l + 1 - 2 * k, 0, 2)
+    near_arrived([0], 2)
+    near_arrived([0], 3)
+    some(PARTNER, other, 2, 4)
     add_up(1)
     send_near([1, 2], 2)
-    forward(0)
-    near_arrived([0], 2)
-    near_arrived([0], 3)
-    some(PARTNER, l + 1 - 2 * k, 2, 3)
-    stage(0)
-
+
+    def pick(i, carry):
+        for j in range(8):
+            out[pl.ds(i * 8 + j, 1), :] = target[pl.ds(ordering[0, i * 8 + j], 1), :]
+        return carry
+
+    lax.fori_loop(0, LEAF // 8, pick, 0)
     add_up(2)
     gather_copy(1).wait_recv()
     gather_copy(2).start()
     send_near([1, 2], 3)
-    forward(1)
-    some(PARTNER, l + 1 - 2 * k, 3, 4)
-    stage(1)
-
+    stage(0)
     add_up(3)
-    forward(2)
     gather_copy(2).wait_recv()
     for i in range(1, 4):
         for copy in row_copies(i):
@@ -277,8 +274,7 @@
     for i in range(1, 4):
         far_out[i - 1] = far_total[i].astype(BF16)
         far_copy(i).start()
-    stage(2)
-
+    stage(1)
     upper = add_up(4).astype(BF16)
     cluster_cols = cluster_skel[0].astype(F32)
     fill_stationary(cluster_at, (cluster_cols + cluster_cols).astype(BF16))
@@ -294,14 +290,7 @@
 
     for i in range(3):
         y_copy(i).start()
-    forward(3)
-
-    def pick(i, carry):
-        for j in range(8):
-            out[pl.ds(i * 8 + j, 1), :] = target[pl.ds(ordering[0, i * 8 + j], 1), :]
-        return carry
-
-    lax.fori_loop(0, LEAF // 8, pick, 0)
+    stage(2)
     for i in range(3):
         y_copy(i).wait_recv()
     lower = jnp.zeros((half, RANK), F32)
@@ -317,6 +306,12 @@
     low_copy.start()
     stage(3)
 
+    def last(c, carry):
+        near_copy(5, c).wait_recv()
+        near_chunk(FAR_SIDE, c, l + 6 * k - 3)
+        return carry
+
+    lax.fori_loop(0, CHUNKS, last, 0)
     for i in range(1, 4):
         far_copy(i).wait_recv()
     low_copy.wait_recv()
@@ -327,12 +322,6 @@
     )
     local = local_t.astype(BF16).astype(F32).T.astype(BF16)
 
-    def last(c, carry):
-        near_copy(5, c).wait_recv()
-        near_chunk(FAR_SIDE, c, l + 6 * k - 3)
-        return carry
-
-    lax.fori_loop(0, CHUNKS, last, 0)
     for i in range(LEAF // LANES):
         rows = slice(i * LANES, (i + 1) * LANES)
         image = dot(basis[rows, :], local) + near[:, rows].T

time: 65.5 us -> 61.9 us (0.945)
  Pallas kernels: 63.1 us -> 59.5 us
    pallas_call x1, Pallas kernels: 63.1 us -> 59.5 us  [body(): pl.pallas_call(kernel, out_shape=jax.ShapeDtypeStruct((LEAF, NRHS), F32),...]
where the time goes in v2:
time: 61.9 us; the launch traced here: 61.8 us
  Pallas kernels  59.5 us (96%)
  local copies, waits for them, and re-layouts  2.26 us (4%)
    pallas_call x1, Pallas kernels, body(): pl.pallas_call(kernel, out_shape=jax.ShapeDtypeStruct((LEAF, NRHS), F32),...  59.5 us
    unnamed x1, local copies, waits for them, and re-layouts  2.26 us

profile of v2, /device:TPU:1, one launch (start us, length us, event | category | flops | bytes accessed | tf_op | source)
XLA Modules:
  0.0 61.8 jit_solution(9386859072315413778)
XLA Ops:
  0.0 59.5 %shard_map.118 = f32[2048,128]{1,0:T(8,128)} custom-call(bf16[64,2048]{1,0:T(8,128)(2,1)} %bitcast.4, s32[1,2048]{1,0:T(1,128)} %ordering.1, f32[2048,128]{1,0:T(8,128)} %iterate.1, f32[2048,128]{1,0:T(8,128)} %target.1, f32[1,128]{1,0:T(1,128)} %bitcast.7, bf16[2048,256]{1,0:T(8,128)(2,1)} %basis.1, bf16[1,256,256]{2,1,0:T(8,128)(2,1)} %transfer.1, ...), custom_call_target="tpu_custom_call" | custom-call | tf_op jit(solution)/shard_map/pallas_call | solution.py:351
  59.5 2.3 %copy.14 = f32[2048,128]{1,0:T(8,128)} copy(f32[2048,128]{1,0:T(8,128)} %shard_map.118) | data formatting | bytes 2097152
